TPU v7x, 32 devices: a whole 2x2x4 slice. The times are simulated.
32 devices in a mesh: gx: 4 (over y, core), gy: 2 (over x), gz: 4 (over z).
Axes of the slice: x: 2, y: 2, z: 4, core: 2. Of those that a mesh axis runs over, the one named last changes fastest.
Arguments:
- right_side: float32 [64, 1024, 256], P('gz', 'gx', 'gy'), may hold values from -8 to 8
- diagonal: float32 [64, 1024, 256], P('gz', 'gx', 'gy'), may hold values from 0.02 to 1
- regime: int32 [1024, 256], P('gx', 'gy'), may hold values from 0 to 7
- inverses: float32 [8, 64, 64], replicated, as said below
Outputs:
- solution: float32 [64, 1024, 256], P('gz', 'gx', 'gy')
- residual: float32 [64, 1024, 256], P('gz', 'gx', 'gy')
Inputs may be any that keep to these rules, and one draw needn't show every extreme that they name: `inverses`: each block is symmetric positive definite.
All inputs are finite; a program needn't handle non-finite values.
Results may differ from a plain program's by a relative error of at most 0.00025.
Values sent between devices are 32-bit elements; how exact they have to be, the bound alone decides.
A program may use at most 128 MiB of HBM per device.

v0:
```python
import jax
import jax.numpy as jnp
from jax import lax
from jax.sharding import PartitionSpec as P

NREG = 8
ITERS = 3


def extended(cells, sides, width):
    for axis, dim in sides:
        count = lax.axis_size(axis)
        ends = count - 1
        head = lax.slice_in_dim(cells, 0, width, axis=dim)
        tail = lax.slice_in_dim(cells, cells.shape[dim] - width, cells.shape[dim], axis=dim)
        cells = jnp.concatenate(
            [
                lax.ppermute(tail, axis, [(i, (i + 1) % count) for i in range(ends)]),
                cells,
                lax.ppermute(head, axis, [((i + 1) % count, i) for i in range(ends)]),
            ],
            axis=dim,
        )
    return cells


def stencil(padded, grid_field, diagonal):
    beside = padded[2:, 1:-1, 1:-1] + padded[:-2, 1:-1, 1:-1]
    beside = beside + padded[1:-1, 2:, 1:-1] + padded[1:-1, :-2, 1:-1]
    beside = beside + padded[1:-1, 1:-1, 2:] + padded[1:-1, 1:-1, :-2]
    return (6.0 + diagonal) * grid_field - beside


def operate(grid_field, diagonal):
    flat_pad = extended(grid_field, ((("gx", "gz"), 1), ("gy", 2)), 1)
    padded = jnp.pad(flat_pad, ((1, 1), (0, 0), (0, 0)))
    return stencil(padded, grid_field, diagonal)


def apply_blocks(matrices, flattened, chosen):
    result = jnp.zeros((matrices.shape[1], flattened.shape[1]), jnp.float32)
    for member in range(NREG):
        product = jnp.dot(matrices[member], flattened, precision=lax.Precision.HIGHEST)
        result = result + jnp.where(chosen[None, :] == member, product, jnp.zeros_like(product))
    return result


def precondition(grid_field, regime, inverses):
    layers = grid_field.shape[0]
    share_rows = grid_field.shape[1]
    offset = lax.axis_index("gz") * share_rows
    chosen = lax.dynamic_slice_in_dim(regime, offset, share_rows, 0).reshape(-1)
    result = apply_blocks(inverses, grid_field.reshape(layers, -1), chosen)
    return result.reshape(grid_field.shape)


def fitness(residual, precond):
    return lax.psum(jnp.sum(residual * precond), ("gx", "gy", "gz"))


def per_device(right_side, diagonal, regime, inverses):
    right_side, diagonal = (
        lax.all_to_all(right_side, "gz", split_axis=1, concat_axis=0, tiled=True),
        lax.all_to_all(diagonal, "gz", split_axis=1, concat_axis=0, tiled=True),
    )
    solution = jnp.zeros_like(right_side)
    residual = right_side
    precond = precondition(residual, regime, inverses)
    inner_rz = fitness(residual, precond)
    search = precond
    for iteration in range(ITERS):
        image = operate(search, diagonal)
        step_len = inner_rz / lax.psum(jnp.sum(search * image), ("gx", "gy", "gz"))
        solution = solution + step_len * search
        residual = residual - step_len * image
        if iteration + 1 < ITERS:
            precond = precondition(residual, regime, inverses)
            rz_next = fitness(residual, precond)
            search = precond + rz_next / inner_rz * search
            inner_rz = rz_next
    solution, residual = (
        lax.all_to_all(solution, "gz", split_axis=0, concat_axis=1, tiled=True),
        lax.all_to_all(residual, "gz", split_axis=0, concat_axis=1, tiled=True),
    )
    return (solution, residual)


def solution(mesh):
    in_specs = (P("gz", "gx", "gy"), P("gz", "gx", "gy"), P("gx", "gy"), P())
    out_specs = (P("gz", "gx", "gy"), P("gz", "gx", "gy"))
    return jax.shard_map(
        per_device, mesh=mesh, in_specs=in_specs, out_specs=out_specs, check_vma=False
    )
```

profile of v0, /device:TPU:0, one launch (start us, length us, event | category | flops | bytes accessed | tf_op | source)
XLA Modules:
  0.0 728.7 jit_solution(265791488601582575)
XLA Ops:
  0.6 4.1 copy.52
  4.8 6.3 all-to-all-start
  15.2 44.1 %all-to-all-done = f32[16,256,128]{2,0,1:T(8,128)S(1)} async-done(((f32[16,256,128]{2,0,1:T(8,128)}), f32[16,256,128]{2,0,1:T(8,128)S(1)}, u32[]{:S(2)}, u32[]{:S(2)}) %all-to-all-start) | async-done | bytes 2097184 | tf_op jit(solution)/shard_map/all_to_all | solution.py:63
  59.3 5.0 all-to-all-start.1
  95.2 4.5 collective-permute-start
  99.7 12.9 %all-to-all-done.1 = f32[16,256,128]{2,0,1:T(8,128)} async-done(((f32[16,256,128]{2,0,1:T(8,128)}), f32[16,256,128]{2,0,1:T(8,128)}, u32[]{:S(2)}, u32[]{:S(2)}) %all-to-all-start.1) | async-done | bytes 2097184 | tf_op jit(solution)/shard_map/all_to_all | solution.py:64
  115.7 5.6 copy.66
  121.2 4.4 copy.59
  125.7 4.4 copy.61
  132.5 4.5 collective-permute-start.2
  138.5 5.6 copy.55
  144.0 4.5 copy.68
  148.6 10.2 %select_maximum_fusion.8 = f32[66,66,130]{1,0,2:T(8,128)} fusion(f32[64,66,1]{1,0,2:T(8,128)S(1)} %collective-permute-done.3, f32[64,66,1]{1,0,2:T(8,128)S(1)} %collective-permute-done.2, f32[64,1,128]{1,0,2:T(8,128)} %copy.61, f32[64,64,128]{1,0,2:T(8,128)} %copy.66, f32[64,1,128]{1,0,2:T(8,128)} %copy.59), kind=kLoop, calls=%fused_computation.55 | loop fusion | flops 6795360 | bytes 4461600 | tf_op jit(solution)/shard_map/concatenate | solution.py:16
  158.8 15.3 %multiply_reduce_fusion.4 = (f32[]{:T(128)}, f32[64,64,128]{1,0,2:T(8,128)}) fusion(f32[64,64,128]{1,0,2:T(8,128)S(1)} %copy-done.4, f32[64,1,128]{1,0,2:T(8,128)S(1)} %copy-done.6, f32[64,1,128]{1,0,2:T(8,128)S(1)} %copy-done.5, f32[64,66,1]{1,0,2:T(8,128)S(1)} %collective-permute-done.2, f32[64,66,1]{1,0,2:T(8,128)S(1)} %collective-permute-done.3, ...), kind=kLoop, calls=%fused_computation.115 | loop fusion | flops 8912895 | bytes 10585092 | tf_op jit(solution)/shard_map/reduce_sum | solution.py:73
  174.1 37.1 %all-reduce.3 = (f32[]{:T(128)}, f32[]{:T(128)}) all-reduce(f32[]{:T(128)} %fusion.53, f32[]{:T(128)} %get-tuple-element.8), channel_id=1, replica_groups=mesh['gx'=4,'gy'=2,'gz'=4] {'gx','gy','gz'}, use_global_device_ids=true, to_apply=%region_1.2 | all-reduce | flops 2 | bytes 16 | tf_op jit(solution)/shard_map/psum | solution.py:58
  212.5 6.9 bitcast_subtract_fusion
  251.7 4.5 copy.70
  256.2 5.1 multiply_reduce_fusion.3
  261.4 42.3 %psum.44 = f32[]{:T(128)} all-reduce(f32[]{:T(128)} %multiply_reduce_fusion.3), channel_id=1, replica_groups=mesh['gx'=4,'gy'=2,'gz'=4] {'gx','gy','gz'}, use_global_device_ids=true, to_apply=%region_5.6 | all-reduce | flops 1 | bytes 8 | tf_op jit(solution)/shard_map/psum | solution.py:58
  305.1 4.4 multiply_add_fusion.2
  309.5 4.6 fusion.147
  324.8 4.6 copy.75
  329.4 4.4 copy.76
  336.5 4.8 collective-permute-start.6
  342.9 7.1 select_maximum_fusion.4
  349.9 15.3 %multiply_reduce_fusion.2 = (f32[]{:T(128)}, f32[64,64,128]{1,0,2:T(8,128)}) fusion(f32[64,64,128]{1,0,2:T(8,128)S(1)} %copy-done.1, f32[64,1,128]{1,0,2:T(8,128)S(1)} %copy-done.10, f32[64,1,128]{1,0,2:T(8,128)S(1)} %copy-done.8, f32[64,66,1]{1,0,2:T(8,128)S(1)} %collective-permute-done.6, f32[64,66,1]{1,0,2:T(8,128)S(1)} %collective-permute-done.7, ...), kind=kLoop, calls=%fused_computation.112 | loop fusion | flops 8912895 | bytes 10585092 | tf_op jit(solution)/shard_map/reduce_sum | solution.py:73
  365.2 44.7 %psum.45 = f32[]{:T(128)} all-reduce(f32[]{:T(128)} %get-tuple-element.6), channel_id=1, replica_groups=mesh['gx'=4,'gy'=2,'gz'=4] {'gx','gy','gz'}, use_global_device_ids=true, to_apply=%region_7.8 | all-reduce | flops 1 | bytes 8 | tf_op jit(solution)/shard_map/psum | solution.py:73
  411.2 6.9 multiply_subtract_fusion.1
  418.0 4.2 copy.79
  450.3 4.5 copy.80
  454.8 5.1 multiply_reduce_fusion.1
  460.0 41.3 %psum.46 = f32[]{:T(128)} all-reduce(f32[]{:T(128)} %multiply_reduce_fusion.1), channel_id=1, replica_groups=mesh['gx'=4,'gy'=2,'gz'=4] {'gx','gy','gz'}, use_global_device_ids=true, to_apply=%region_9.10 | all-reduce | flops 1 | bytes 8 | tf_op jit(solution)/shard_map/psum | solution.py:58
  502.7 4.4 multiply_add_fusion.1
  507.1 4.7 fusion.146
  522.4 4.9 copy.84
  527.3 4.4 copy.85
  534.4 4.8 collective-permute-start.10
  540.8 7.1 select_maximum_fusion
  547.9 15.3 %multiply_reduce_fusion = (f32[]{:T(128)}, f32[64,64,128]{1,0,2:T(8,128)}) fusion(f32[64,64,128]{1,0,2:T(8,128)S(1)} %copy-done.3, f32[64,1,128]{1,0,2:T(8,128)S(1)} %copy-done.9, f32[64,1,128]{1,0,2:T(8,128)S(1)} %copy-done.7, f32[64,66,1]{1,0,2:T(8,128)S(1)} %collective-permute-done.10, f32[64,66,1]{1,0,2:T(8,128)S(1)} %collective-permute-done.11, ...), kind=kLoop, calls=%fused_computation.108 | loop fusion | flops 8912895 | bytes 10585092 | tf_op jit(solution)/shard_map/reduce_sum | solution.py:73
  563.3 45.1 %psum.47 = f32[]{:T(128)} all-reduce(f32[]{:T(128)} %get-tuple-element.4), channel_id=1, replica_groups=mesh['gx'=4,'gy'=2,'gz'=4] {'gx','gy','gz'}, use_global_device_ids=true, to_apply=%region_11.12 | all-reduce | flops 1 | bytes 8 | tf_op jit(solution)/shard_map/psum | solution.py:73
  609.7 6.9 multiply_subtract_fusion
  616.5 4.8 copy.90
  621.3 4.2 all-to-all-start.3
  625.5 8.6 %multiply_add_fusion = f32[64,64,128]{1,0,2:T(8,128)} fusion(f32[64,64,128]{1,0,2:T(8,128)} %copy-done.2, f32[64,64,128]{1,0,2:T(8,128)} %copy-done, f32[64,64,128]{1,0,2:T(8,128)} %copy.66, f32[]{:T(128)S(6)} %div.19, f32[]{:T(128)S(6)} %div.17, f32[]{:T(128)S(6)} %div.15), kind=kLoop, calls=%fused_computation.107 | loop fusion | flops 2621440 | bytes 8388620 | tf_op jit(solution)/shard_map/add | solution.py:74
  634.1 4.8 copy.88
  638.9 34.2 %all-to-all-done.3 = f32[64,64,128]{2,1,0:T(8,128)S(1)} async-done(((f32[64,64,128]{2,1,0:T(8,128)}), f32[64,64,128]{2,1,0:T(8,128)S(1)}, u32[]{:S(2)}, u32[]{:S(2)}) %all-to-all-start.3) | async-done | bytes 2097184 | tf_op jit(solution)/shard_map/all_to_all | solution.py:83
  673.1 4.5 all-to-all-start.2
  679.0 46.4 %all-to-all-done.2 = f32[64,64,128]{2,1,0:T(8,128)} async-done(((f32[64,64,128]{2,1,0:T(8,128)}), f32[64,64,128]{2,1,0:T(8,128)}, u32[]{:S(2)}, u32[]{:S(2)}) %all-to-all-start.2) | async-done | bytes 2097184 | tf_op jit(solution)/shard_map/all_to_all | solution.py:82
  (91 shorter events, 136.3 us)
Async XLA Ops:
  4.8 54.5 %all-to-all-start = ((f32[16,256,128]{2,0,1:T(8,128)}), f32[16,256,128]{2,0,1:T(8,128)S(1)}, u32[]{:S(2)}, u32[]{:S(2)}) async-start(f32[16,256,128]{2,0,1:T(8,128)} %copy.52), calls=%async_computation | async-start | bytes 4194304 | tf_op jit(solution)/shard_map/all_to_all | solution.py:63
  59.3 53.3 %all-to-all-start.1 = ((f32[16,256,128]{2,0,1:T(8,128)}), f32[16,256,128]{2,0,1:T(8,128)}, u32[]{:S(2)}, u32[]{:S(2)}) async-start(f32[16,256,128]{2,0,1:T(8,128)} %copy.54), calls=%async_computation.1 | async-start | bytes 4194304 | tf_op jit(solution)/shard_map/all_to_all | solution.py:64
  65.1 1.0 copy-start.13
  92.5 1.3 copy-start.11
  93.9 31.8 %collective-permute-start.1 = (f32[64,1,128]{2,0,1:T(8,128)S(1)}, f32[64,1,128]{2,0,1:T(8,128)S(1)}, u32[]{:S(2)}, u32[]{:S(2)}) collective-permute-start(f32[64,1,128]{2,0,1:T(8,128)S(1)} %bitcast.220), channel_id=1, source_target_pairs={{1,0},{2,1},{3,2},{8,3},{9,8},{10,9},{11,10},{16,11},{17,16},{18,1... | collective-permute-start | bytes 98312 | tf_op jit(solution)/shard_map/ppermute | solution.py:20
  95.2 26.1 %collective-permute-start = (f32[64,1,128]{2,0,1:T(8,128)S(1)}, f32[64,1,128]{2,0,1:T(8,128)S(1)}, u32[]{:S(2)}, u32[]{:S(2)}) collective-permute-start(f32[64,1,128]{2,0,1:T(8,128)S(1)} %bitcast.221), channel_id=1, source_target_pairs={{0,1},{1,2},{2,3},{3,8},{8,9},{9,10},{10,11},{11,16},{16,17},{17,1... | collective-permute-start | bytes 98312 | tf_op jit(solution)/shard_map/ppermute | solution.py:18
  130.1 7.0 copy-start.12
  131.2 17.4 %collective-permute-start.3 = (f32[64,66,1]{1,0,2:T(8,128)S(1)}, f32[64,66,1]{1,0,2:T(8,128)S(1)}, u32[]{:S(2)}, u32[]{:S(2)}) collective-permute-start(f32[64,66,1]{1,0,2:T(8,128)S(1)} %get-tuple-element.14), channel_id=1, source_target_pairs={{4,0},{5,1},{6,2},{7,3},{12,8},{13,9},{14,10},{15,11},{20,16},{21,... | collective-permute-start | bytes 50696 | tf_op jit(solution)/shard_map/ppermute | solution.py:20
  132.5 16.1 %collective-permute-start.2 = (f32[64,66,1]{1,0,2:T(8,128)S(1)}, f32[64,66,1]{1,0,2:T(8,128)S(1)}, u32[]{:S(2)}, u32[]{:S(2)}) collective-permute-start(f32[64,66,1]{1,0,2:T(8,128)S(1)} %get-tuple-element.15), channel_id=1, source_target_pairs={{0,4},{1,5},{2,6},{3,7},{8,12},{9,13},{10,14},{11,15},{16,20},{17,... | collective-permute-start | bytes 50696 | tf_op jit(solution)/shard_map/ppermute | solution.py:18
  148.6 10.2 %copy-start.4 = (f32[64,64,128]{1,0,2:T(8,128)S(1)}, f32[64,64,128]{1,0,2:T(8,128)}, u32[]{:S(2)}) copy-start(f32[64,64,128]{1,0,2:T(8,128)} %copy.66) | copy-start | bytes 6291460
  148.6 10.2 %copy-start.5 = (f32[64,1,128]{1,0,2:T(8,128)S(1)}, f32[64,1,128]{1,0,2:T(8,128)}, u32[]{:S(2)}) copy-start(f32[64,1,128]{1,0,2:T(8,128)} %copy.59) | copy-start | bytes 98308
  148.6 10.2 %copy-start.6 = (f32[64,1,128]{1,0,2:T(8,128)S(1)}, f32[64,1,128]{1,0,2:T(8,128)}, u32[]{:S(2)}) copy-start(f32[64,1,128]{1,0,2:T(8,128)} %copy.61) | copy-start | bytes 98308
  309.5 4.6 copy-start
  317.9 6.9 collective-permute-start.4
  323.5 5.9 collective-permute-start.5
  333.8 9.1 %copy-start.1 = (f32[64,64,128]{1,0,2:T(8,128)S(1)}, f32[64,64,128]{1,0,2:T(8,128)}, u32[]{:S(2)}) copy-start(f32[64,64,128]{1,0,2:T(8,128)} %copy-done) | copy-start | bytes 6291460
  333.8 9.1 %copy-start.8 = (f32[64,1,128]{1,0,2:T(8,128)S(1)}, f32[64,1,128]{1,0,2:T(8,128)}, u32[]{:S(2)}) copy-start(f32[64,1,128]{1,0,2:T(8,128)} %copy.75) | copy-start | bytes 98308
  333.8 9.1 %copy-start.10 = (f32[64,1,128]{1,0,2:T(8,128)S(1)}, f32[64,1,128]{1,0,2:T(8,128)}, u32[]{:S(2)}) copy-start(f32[64,1,128]{1,0,2:T(8,128)} %copy.76) | copy-start | bytes 98308
  334.9 6.4 collective-permute-start.7
  336.5 6.4 collective-permute-start.6
  507.1 4.7 copy-start.2
  515.5 6.9 collective-permute-start.8
  521.1 6.2 collective-permute-start.9
  531.8 9.1 %copy-start.3 = (f32[64,64,128]{1,0,2:T(8,128)S(1)}, f32[64,64,128]{1,0,2:T(8,128)}, u32[]{:S(2)}) copy-start(f32[64,64,128]{1,0,2:T(8,128)} %copy-done.2) | copy-start | bytes 6291460
  531.8 9.1 %copy-start.7 = (f32[64,1,128]{1,0,2:T(8,128)S(1)}, f32[64,1,128]{1,0,2:T(8,128)}, u32[]{:S(2)}) copy-start(f32[64,1,128]{1,0,2:T(8,128)} %copy.84) | copy-start | bytes 98308
  531.8 9.1 %copy-start.9 = (f32[64,1,128]{1,0,2:T(8,128)S(1)}, f32[64,1,128]{1,0,2:T(8,128)}, u32[]{:S(2)}) copy-start(f32[64,1,128]{1,0,2:T(8,128)} %copy.85) | copy-start | bytes 98308
  532.9 6.4 collective-permute-start.11
  534.4 6.4 collective-permute-start.10
  621.3 51.8 %all-to-all-start.3 = ((f32[64,64,128]{2,1,0:T(8,128)}), f32[64,64,128]{2,1,0:T(8,128)S(1)}, u32[]{:S(2)}, u32[]{:S(2)}) async-start(f32[64,64,128]{2,1,0:T(8,128)} %copy.90), calls=%async_computation.3 | async-start | bytes 4194304 | tf_op jit(solution)/shard_map/all_to_all | solution.py:83
  673.1 52.3 %all-to-all-start.2 = ((f32[64,64,128]{2,1,0:T(8,128)}), f32[64,64,128]{2,1,0:T(8,128)}, u32[]{:S(2)}, u32[]{:S(2)}) async-start(f32[64,64,128]{2,1,0:T(8,128)} %copy.88), calls=%async_computation.2 | async-start | bytes 4194304 | tf_op jit(solution)/shard_map/all_to_all | solution.py:82
where the time goes:
time: 733 us; the launch traced here: 729 us
  blocking collectives  211 us (29%)
  waiting for transfers between devices  141 us (19%)
  other arithmetic  127 us (17%)
  local copies, waits for them, and re-layouts  110 us (15%)
  matrix products  81.5 us (11%)
  starting transfers between devices  50.6 us (7%)
  between operations  8.02 us (1%)
    psum x3, blocking collectives, fitness(): return lax.psum(jnp.sum(residual * precond), ('gx', 'gy', 'gz'))  121 us
    psum x2, blocking collectives, per_device(): step_len = inner_rz / lax.psum(jnp.sum(search * image), ('gx', 'gy', 'gz'))  89.7 us
    dot_general x24, matrix products, apply_blocks(): jnp.dot(matrices[member], flattened, precision=lax.Precision.HIGHEST)  81.5 us
    all_to_all x1, waiting for transfers between devices, per_device(): lax.all_to_all(solution, 'gz', split_axis=0, concat_axis=1, tiled=True)  46.4 us
    reduce_sum x3, other arithmetic, per_device(): step_len = inner_rz / lax.psum(jnp.sum(search * image), ('gx', 'gy', 'gz'))  46 us
    all_to_all x1, waiting for transfers between devices, per_device(): lax.all_to_all(right_side, 'gz', split_axis=1, concat_axis=0, tiled=True)  44.1 us
    all_to_all x1, waiting for transfers between devices, per_device(): lax.all_to_all(residual, 'gz', split_axis=0, concat_axis=1, tiled=True)  34.2 us
    concatenate x6, other arithmetic, extended(): jnp.concatenate([lax.ppermute(tail, axis, [(i, (i + 1) % count) for i in...  27.6 us
  transfers between devices with their start and end apart: 16, of which 6 were waited for; matrix products, arithmetic and copies ran while one was open for 12% of the time, Pallas kernels for 0%

commit v1 on v0

v1 whole, which is shorter than its diff:
```python
import functools

import jax
import jax.numpy as jnp
from jax import lax
from jax.experimental import pallas as pl
from jax.experimental.pallas import tpu as pltpu
from jax.sharding import PartitionSpec as P

MESH = pl.DeviceIdType.MESH
BASIS = 3
CHUNKS = 4
SUMS = 16


def kernel(
    sizes,
    rhs,
    diag,
    regime,
    inverses,
    weights,
    x_out,
    r_out,
    rhs_z,
    diag_z,
    rhs_t,
    diag_t,
    fields,
    images,
    edges,
    edges_left,
    edges_right,
    x_z,
    r_z,
    sums_z,
    sums_x,
    sums_y,
    local_sem,
    in_send,
    in_recv,
    halo_send,
    halo_recv,
    sum_send,
    sum_recv,
    out_send,
    out_recv,
    out_local,
):
    nx, ny, nz = sizes["gx"], sizes["gy"], sizes["gz"]
    mx, my, mz = lax.axis_index("gx"), lax.axis_index("gy"), lax.axis_index("gz")
    slab = rhs.shape[0]
    depth = slab * nz
    rows = rhs.shape[1] // nz
    lanes = rhs.shape[2]
    nreg = inverses.shape[0]

    even = lax.rem(mx, 2) == 0

    def place(z):
        return jnp.where(even, z, nz - 1 - z)

    mine = place(mz)

    def row_span(z, start, count):
        return pl.ds(pl.multiple_of(place(z) * rows + start, 8), count)

    def slab_span(z):
        return pl.ds(z * slab, slab)

    axes = (("gx", nx, mx), ("gy", ny, my), ("gz", nz, mz))
    barrier = pltpu.get_barrier_semaphore()
    for name, count, me in axes:
        for k in range(1, count):
            pl.semaphore_signal(
                barrier, inc=1, device_id={name: lax.rem(me + k, count)}, device_id_type=MESH
            )
    pl.semaphore_wait(barrier, nx + ny + nz - 3)

    def slab_in(which, source, target, k, peer, span_owner):
        return pltpu.make_async_remote_copy(
            src_ref=source.at[:, row_span(peer, 0, rows), :],
            dst_ref=target.at[slab_span(span_owner)],
            send_sem=in_send.at[which, k],
            recv_sem=in_recv.at[which, k],
            device_id={"gz": peer},
            device_id_type=MESH,
        )

    pairs = ((rhs, rhs_z), (diag, diag_z))
    for which, (source, target) in enumerate(pairs):
        for k in (list(range(1, nz))):
            slab_in(which, source, target, k, lax.rem(mz + k, nz), mz).start()
        pltpu.make_async_copy(
            source.at[:, row_span(mz, 0, rows), :], target.at[slab_span(mz)], local_sem.at[which]
        ).start()

    def slab_wait(which):
        source, target = pairs[which]
        pltpu.make_async_copy(
            source.at[:, row_span(mz, 0, rows), :], target.at[slab_span(mz)], local_sem.at[which]
        ).wait()
        for k in range(1, nz):
            sender = lax.rem(mz + nz - k, nz)
            slab_in(which, source, target, k, sender, sender).wait_recv()

    blocks = inverses[...]
    scale = 1.0 / jnp.max(jnp.max(jnp.abs(blocks), axis=0), axis=(0, 1), keepdims=True)
    total = jnp.sum(blocks, axis=0)
    on_diagonal = lax.broadcasted_iota(jnp.int32, total.shape, 0) == lax.broadcasted_iota(
        jnp.int32, total.shape, 1
    )
    trace = jnp.sum(jnp.where(on_diagonal, total, 0.0), axis=(0, 1), keepdims=True)
    shift = scale * trace * (6.0 / (nreg * depth))

    lane = lax.broadcasted_iota(jnp.int32, (depth, lanes), 1)
    layer = lax.broadcasted_iota(jnp.int32, (depth, lanes), 0)
    zeros = jnp.zeros((depth, lanes), jnp.float32)

    has_prev = jnp.logical_or(mine > 0, mx > 0)
    has_next = jnp.logical_or(mine < nz - 1, mx < nx - 1)
    has_left = my > 0
    has_right = my < ny - 1
    step_z = jnp.where(even, 1, -1)
    at_top, at_end = mine == 0, mine == nz - 1
    prev_id = {
        "gx": jnp.where(at_top, jnp.maximum(mx - 1, 0), mx),
        "gz": jnp.where(at_top, mz, mz - step_z),
    }
    next_id = {
        "gx": jnp.where(at_end, jnp.minimum(mx + 1, nx - 1), mx),
        "gz": jnp.where(at_end, mz, mz + step_z),
    }
    left_id = {"gy": jnp.maximum(my - 1, 0)}
    right_id = {"gy": jnp.minimum(my + 1, ny - 1)}

    def halo(n):
        rows_of = fields.at[n]
        return (
            (has_prev, has_next, rows_of.at[1], rows_of.at[rows + 1], prev_id),
            (has_next, has_prev, rows_of.at[rows], rows_of.at[0], next_id),
            (has_left, has_right, edges.at[n], edges_right.at[n], left_id),
            (has_right, has_left, edges.at[n], edges_left.at[n], right_id),
        )

    def halo_copy(n, at, source, target, device):
        return pltpu.make_async_remote_copy(
            src_ref=source,
            dst_ref=target,
            send_sem=halo_send.at[n, at],
            recv_sem=halo_recv.at[n, at],
            device_id=device,
            device_id_type=MESH,
        )

    for n in range(BASIS):
        for _, gets, _, target, _ in halo(n):

            @pl.when(jnp.logical_not(gets))
            def _(target=target):
                target[...] = zeros

    def precondition(n):
        edges[n] = zeros

        def body(b, carry):
            columns = []
            for half in range(2):
                i = 2 * b + half
                if n == 0:
                    column = rhs_z.reshape(depth * rows, lanes)[pl.ds(i, depth, stride=rows), :]
                    rhs_t[i] = column
                else:
                    column = images[n - 1, i]
                columns.append(column)
            wide = jnp.concatenate(columns, axis=1)
            high = wide.astype(jnp.bfloat16)
            low = (wide - high.astype(jnp.float32)).astype(jnp.bfloat16)
            stacked = jnp.concatenate([high, high, low], axis=0)
            product = jnp.dot(weights[...], stacked, preferred_element_type=jnp.float32)
            packed = edges[n]
            for half in range(2):
                i = 2 * b + half
                chosen = jnp.broadcast_to(
                    regime[pl.ds(mine * rows + i, 1), :], (depth, lanes)
                )
                span = slice(half * lanes, (half + 1) * lanes)
                picked = product[:depth, span]
                for member in range(1, nreg):
                    part = product[member * depth : (member + 1) * depth, span]
                    picked = jnp.where(chosen == member, part, picked)
                value = picked * scale
                if n > 0:
                    value = value - shift * fields[n - 1, i + 1]
                fields[n, i + 1] = value
                packed = jnp.where(lane == i, pltpu.roll(value, i, 1), packed)
                packed = jnp.where(
                    lane == rows + i, pltpu.roll(value, lax.rem(rows + i + 1, lanes), 1), packed
                )
            edges[n] = packed
            return carry

        lax.fori_loop(0, rows // 2, body, 0)
        for at, (sends, _, source, target, device) in enumerate(halo(n)):

            @pl.when(sends)
            def _(at=at, source=source, target=target, device=device):
                halo_copy(n, at, source, target, device).start()

    def halo_wait(n):
        for at, (_, gets, source, target, device) in enumerate(halo(n)):

            @pl.when(gets)
            def _(at=at, source=source, target=target, device=device):
                halo_copy(n, at, source, target, device).wait_recv()

    def fold(product):
        return jnp.sum(product.reshape(depth // 8, 8, lanes), axis=0)

    def operate(n):
        halo_wait(n)

        def body(i, carry):
            field = fields[n, i + 1]
            if n == 0:
                bulk = diag_z.reshape(depth * rows, lanes)[pl.ds(i, depth, stride=rows), :]
                diag_t[i] = bulk
            else:
                bulk = diag_t[i]
            beside = fields[n, i] + fields[n, i + 2]
            beside = beside + jnp.where(layer == 0, 0.0, pltpu.roll(field, 1, 0))
            beside = beside + jnp.where(layer == depth - 1, 0.0, pltpu.roll(field, depth - 1, 0))
            from_left = pltpu.roll(edges_left[n], lanes - rows - i, 1)
            beside = beside + jnp.where(lane == 0, from_left, pltpu.roll(field, 1, 1))
            from_right = pltpu.roll(edges_right[n], lanes - 1 - i, 1)
            beside = beside + jnp.where(
                lane == lanes - 1, from_right, pltpu.roll(field, lanes - 1, 1)
            )
            image = (6.0 + bulk) * field - beside
            images[n, i] = image
            sums = [fold(rhs_t[i] * field), fold(field * image)]
            for m in range(n):
                sums.append(fold(fields[m, i + 1] * image))
            return tuple(old + new for old, new in zip(carry, sums))

        start = tuple(jnp.zeros((8, lanes), jnp.float32) for _ in range(n + 2))
        parts = lax.fori_loop(0, rows, body, start)
        return [jnp.sum(part, axis=0, keepdims=True) for part in parts]

    slab_wait(0)
    precondition(0)
    slab_wait(1)
    sums = operate(0)
    precondition(1)
    sums = sums + operate(1)
    precondition(2)
    sums = sums + operate(2)

    sums.append(jnp.zeros((SUMS - len(sums), lanes), jnp.float32))
    value = jnp.concatenate(sums, axis=0)
    stages = (("gz", nz, mz, sums_z), ("gx", nx, mx, sums_x), ("gy", ny, my, sums_y))
    for stage, (name, count, me, slots) in enumerate(stages):
        slots[me] = value

        def sum_copy(k, peer, owner):
            return pltpu.make_async_remote_copy(
                src_ref=slots.at[me],
                dst_ref=slots.at[owner],
                send_sem=sum_send.at[stage, k],
                recv_sem=sum_recv.at[stage, k],
                device_id={name: peer},
                device_id_type=MESH,
            )

        for k in range(1, count):
            sum_copy(k, lax.rem(me + k, count), me).start()
        for k in range(1, count):
            sender = lax.rem(me + count - k, count)
            sum_copy(k, sender, sender).wait_recv()
        value = slots[0]
        for at in range(1, count):
            value = value + slots[at]
        for k in range(1, count):
            sum_copy(k, lax.rem(me + k, count), me).wait_send()

    def entry(at):
        row = jnp.sum(value[at : at + 1, :], axis=1, keepdims=True)
        return jnp.broadcast_to(row, (8, lanes))

    g0, a00, g1, a11, a01, g2, a22, a02, a12 = [entry(at) for at in range(9)]

    def inverse(pivot, size):
        good = pivot > 1e-7 * size
        return jnp.where(good, 1.0 / jnp.where(good, pivot, 1.0), 0.0)

    p0 = inverse(a00, a00)
    l1, l2 = a01 * p0, a02 * p0
    d1 = a11 - l1 * a01
    e1 = a12 - l2 * a01
    h1 = g1 - l1 * g0
    p1 = inverse(d1, a11)
    l21 = e1 * p1
    d2 = a22 - l2 * a02 - l21 * e1
    h2 = g2 - l2 * g0 - l21 * h1
    c2 = h2 * inverse(d2, a22)
    c1 = (h1 - e1 * c2) * p1
    c0 = (g0 - a01 * c1 - a02 * c2) * p0
    c0, c1, c2 = (c[0:1] for c in (c0, c1, c2))

    piece = rows // CHUNKS
    outs = ((x_z, x_out), (r_z, r_out))

    def slab_out(which, chunk, k, peer, owner):
        source, target = outs[which]
        return pltpu.make_async_remote_copy(
            src_ref=source.at[slab_span(peer), pl.ds(chunk * piece, piece), :],
            dst_ref=target.at[:, row_span(owner, chunk * piece, piece), :],
            send_sem=out_send.at[which, chunk, k],
            recv_sem=out_recv.at[which, chunk, k],
            device_id={"gz": peer},
            device_id_type=MESH,
        )

    def keep(which, chunk):
        source, target = outs[which]
        return pltpu.make_async_copy(
            source.at[slab_span(mz), pl.ds(chunk * piece, piece), :],
            target.at[:, row_span(mz, chunk * piece, piece), :],
            out_local.at[which, chunk],
        )

    for chunk in range(CHUNKS):

        def final(i, carry):
            i = chunk * piece + i
            span = pl.ds(i, depth, stride=rows)
            x = c0 * fields[0, i + 1] + c1 * fields[1, i + 1] + c2 * fields[2, i + 1]
            x_z.reshape(depth * rows, lanes)[span, :] = x
            r = rhs_t[i] - (c0 * images[0, i] + c1 * images[1, i] + c2 * images[2, i])
            r_z.reshape(depth * rows, lanes)[span, :] = r
            return carry

        lax.fori_loop(0, piece, final, 0)
        for which in range(2):
            for k in range(1, nz):
                slab_out(which, chunk, k, lax.rem(mz + k, nz), mz).start()
            keep(which, chunk).start()

    for which, (source, target) in enumerate(pairs):
        for k in range(1, nz):
            slab_in(which, source, target, k, lax.rem(mz + k, nz), mz).wait_send()
    for n in range(BASIS):
        for at, (sends, _, source, target, device) in enumerate(halo(n)):

            @pl.when(sends)
            def _(n=n, at=at, source=source, target=target, device=device):
                halo_copy(n, at, source, target, device).wait_send()

    for which in range(2):
        for chunk in range(CHUNKS):
            keep(which, chunk).wait()
            for k in range(1, nz):
                sender = lax.rem(mz + nz - k, nz)
                slab_out(which, chunk, k, sender, sender).wait_recv()
                slab_out(which, chunk, k, lax.rem(mz + k, nz), mz).wait_send()


def per_device(sizes, right_side, diagonal, regime, inverses):
    slab, wide, lanes = right_side.shape
    nz = sizes["gz"]
    depth, rows = slab * nz, wide // nz
    nreg = inverses.shape[0]
    high = lax.reduce_precision(inverses, 8, 7)
    low = lax.reduce_precision(inverses - high, 8, 7)
    weights = jnp.concatenate([high, low, high], axis=-1).reshape(nreg * depth, 3 * depth)
    weights = weights.astype(jnp.bfloat16)
    column = (rows, depth, lanes)
    layered = (depth, rows, lanes)
    f32 = jnp.float32
    dma = pltpu.SemaphoreType.DMA
    return pl.pallas_call(
        functools.partial(kernel, sizes),
        out_shape=[jax.ShapeDtypeStruct(right_side.shape, f32)] * 2,
        in_specs=[pl.BlockSpec(memory_space=pl.ANY)] * 2
        + [pl.BlockSpec(memory_space=pltpu.VMEM)] * 3,
        out_specs=[pl.BlockSpec(memory_space=pl.ANY)] * 2,
        scratch_shapes=[
            pltpu.VMEM(layered, f32),
            pltpu.VMEM(layered, f32),
            pltpu.VMEM(column, f32),
            pltpu.VMEM(column, f32),
            pltpu.VMEM((BASIS, rows + 2, depth, lanes), f32),
            pltpu.VMEM((BASIS, rows, depth, lanes), f32),
            pltpu.VMEM((BASIS, depth, lanes), f32),
            pltpu.VMEM((BASIS, depth, lanes), f32),
            pltpu.VMEM((BASIS, depth, lanes), f32),
            pltpu.VMEM(layered, f32),
            pltpu.VMEM(layered, f32),
            pltpu.VMEM((nz, SUMS, lanes), f32),
            pltpu.VMEM((sizes["gx"], SUMS, lanes), f32),
            pltpu.VMEM((sizes["gy"], SUMS, lanes), f32),
            dma((2,)),
            dma((2, nz)),
            dma((2, nz)),
            dma((BASIS, 4)),
            dma((BASIS, 4)),
            dma((3, max(sizes.values()))),
            dma((3, max(sizes.values()))),
            dma((2, CHUNKS, nz)),
            dma((2, CHUNKS, nz)),
            dma((2, CHUNKS)),
        ],
        compiler_params=pltpu.CompilerParams(
            collective_id=0, has_side_effects=True, vmem_limit_bytes=56 * 1024 * 1024
        ),
    )(right_side, diagonal, regime, inverses, weights)


def solution(mesh):
    sizes = {name: mesh.shape[name] for name in ("gx", "gy", "gz")}
    in_specs = (P("gz", "gx", "gy"), P("gz", "gx", "gy"), P("gx", "gy"), P())
    out_specs = (P("gz", "gx", "gy"), P("gz", "gx", "gy"))
    return jax.shard_map(
        functools.partial(per_device, sizes),
        mesh=mesh,
        in_specs=in_specs,
        out_specs=out_specs,
        check_vma=False,
    )
```

time: 733 us -> 254 us (0.35)
  Pallas kernels: 0 us -> 247 us
  blocking collectives: 211 us -> 0 us
  waiting for transfers between devices: 141 us -> 0 us
  other arithmetic: 127 us -> 1.92 us
  local copies, waits for them, and re-layouts: 110 us -> 4.58 us
  matrix products: 81.5 us -> 0 us
  starting transfers between devices: 50.6 us -> 0 us
  between operations: 8.02 us -> 0.65 us
    pallas_call x0 -> x1, Pallas kernels: none -> 247 us  [per_device(): pl.pallas_call(functools.partial(kernel, sizes), out_shape=[jax.ShapeDtyp...]
    psum x5 -> x0, blocking collectives: 211 us -> none  [the longest x3 121 us: fitness(): return lax.psum(jnp.sum(residual * precond), ('gx', 'gy', 'gz'))]
    all_to_all x4 -> x0, waiting for transfers between devices: 138 us -> none  [the longest x1 46.4 us: per_device(): lax.all_to_all(solution, 'gz', split_axis=0, concat_axis=1, tiled=True)]
    dot_general x24 -> x0, matrix products: 81.5 us -> none  [apply_blocks(): jnp.dot(matrices[member], flattened, precision=lax.Precision.HIGHEST)]
    reduce_sum x6 -> x0, other arithmetic: 57.7 us -> none  [the longest x3 46 us: per_device(): step_len = inner_rz / lax.psum(jnp.sum(search * image), ('gx', 'gy', 'gz'))]
    ppermute x12 -> x0, starting transfers between devices: 30.6 us -> none  [the longest x6 22.4 us: extended(): lax.ppermute(tail, axis, [(i, (i + 1) % count) for i in range(ends)])]
    ppermute x6 -> x0, local copies, waits for them, and re-layouts: 27.2 us -> none  [the longest x3 14 us: extended(): lax.ppermute(tail, axis, [(i, (i + 1) % count) for i in range(ends)])]
    concatenate x6 -> x1, other arithmetic: 27.6 us -> 0.92 us  [per_device(): jnp.concatenate([high, low, high], axis=-1).reshape(nreg * depth, 3 * depth)]
  transfers between devices with their start and end apart: 16 -> 0, of which waited for: 6 -> 0; matrix products, arithmetic and copies ran while one was open for 12% -> 0% of each run, Pallas kernels for 0% -> 0%
where the time goes in v1:
time: 254 us
  Pallas kernels  247 us (97%)
  local copies, waits for them, and re-layouts  4.58 us (2%)
    pallas_call x1, Pallas kernels, per_device(): pl.pallas_call(functools.partial(kernel, sizes), out_shape=[jax.ShapeDtyp...  247 us

profile of v1, /device:TPU:0, one launch (start us, length us, event | category | flops | bytes accessed | tf_op | source)
XLA Modules:
  0.0 253.7 jit_solution(2737393398233133937)
XLA Ops:
  0.6 1.0 fusion.1
  1.6 0.9 pad_maximum_fusion
  2.6 246.5 %shard_map.59 = (f32[16,256,128]{2,1,0:T(8,128)}, f32[16,256,128]{2,1,0:T(8,128)}) custom-call(f32[16,256,128]{2,1,0:T(8,128)} %rhs.1, f32[16,256,128]{2,1,0:T(8,128)} %diag.1, s32[256,128]{1,0:T(8,128)} %regime.1, f32[8,64,64]{2,1,0:T(8,128)} %inverses.1, bf16[512,192]{1,0:T(8,128)(2,1)} %bitcast.1), custom_call_target="tpu_custom_call" | custom-call | tf_op jit(solution)/shard_map/pallas_call | solution.py:381
  249.1 0.0 copy-start
  249.1 3.3 %copy.8 = f32[16,256,128]{2,1,0:T(8,128)} copy(f32[16,256,128]{2,1,0:T(8,128)} %get-tuple-element.6) | data formatting | bytes 4194304
  252.4 0.0 copy-done
  252.4 1.3 copy.9
Async XLA Ops:
  249.1 3.3 %copy-start = (f32[16,256,128]{2,1,0:T(8,128)S(1)}, f32[16,256,128]{2,1,0:T(8,128)}, u32[]{:S(2)}) copy-start(f32[16,256,128]{2,1,0:T(8,128)} %get-tuple-element.7) | copy-start | bytes 6291460

commit v2 on v1

--- a/solution.py
+++ b/solution.py
@@ -11,6 +11,9 @@
 BASIS = 3
 CHUNKS = 4
 SUMS = 16
+UNROLL_M = 2
+UNROLL_A = 4
+UNROLL_F = 4
 
 
 def kernel(
@@ -19,11 +22,13 @@
     diag,
     regime,
     inverses,
-    weights,
     x_out,
     r_out,
+    weights,
     rhs_z,
     diag_z,
+    rhs_slab,
+    diag_slab,
     rhs_t,
     diag_t,
     fields,
@@ -32,7 +37,10 @@
     edges_left,
     edges_right,
     x_z,
-    r_z,
+    x_rim,
+    x_in,
+    rim_in,
+    r_in,
     sums_z,
     sums_x,
     sums_y,
@@ -46,6 +54,9 @@
     out_send,
     out_recv,
     out_local,
+    rim_send,
+    rim_recv,
+    slab_sem,
 ):
     nx, ny, nz = sizes["gx"], sizes["gy"], sizes["gz"]
     mx, my, mz = lax.axis_index("gx"), lax.axis_index("gy"), lax.axis_index("gz")
@@ -77,32 +88,47 @@
             )
     pl.semaphore_wait(barrier, nx + ny + nz - 3)
 
-    def slab_in(which, source, target, k, peer, span_owner):
+    piece = rows // CHUNKS
+    pairs = ((rhs, rhs_z), (diag, diag_z))
+
+    def slab_in(which, chunk, k, peer, owner):
+        source, target = pairs[which]
         return pltpu.make_async_remote_copy(
-            src_ref=source.at[:, row_span(peer, 0, rows), :],
-            dst_ref=target.at[slab_span(span_owner)],
-            send_sem=in_send.at[which, k],
-            recv_sem=in_recv.at[which, k],
+            src_ref=source.at[:, row_span(peer, chunk * piece, piece), :],
+            dst_ref=target.at[slab_span(owner), pl.ds(chunk * piece, piece), :],
+            send_sem=in_send.at[which, chunk, k],
+            recv_sem=in_recv.at[which, chunk, k],
             device_id={"gz": peer},
             device_id_type=MESH,
         )
 
-    pairs = ((rhs, rhs_z), (diag, diag_z))
-    for which, (source, target) in enumerate(pairs):
-        for k in (list(range(1, nz))):
-            slab_in(which, source, target, k, lax.rem(mz + k, nz), mz).start()
-        pltpu.make_async_copy(
+    def own_in(which):
+        source, target = pairs[which]
+        return pltpu.make_async_copy(
             source.at[:, row_span(mz, 0, rows), :], target.at[slab_span(mz)], local_sem.at[which]
-        ).start()
-
-    def slab_wait(which):
-        source, target = pairs[which]
-        pltpu.make_async_copy(
-            source.at[:, row_span(mz, 0, rows), :], target.at[slab_span(mz)], local_sem.at[which]
-        ).wait()
+        )
+
+    slabs = ((rhs, rhs_slab), (diag, diag_slab))
+    for which in range(2):
+        for chunk in range(CHUNKS):
+            for k in range(1, nz):
+                slab_in(which, chunk, k, lax.rem(mz + k, nz), mz).start()
+        own_in(which).start()
+    for which, (source, target) in enumerate(slabs):
+        pltpu.make_async_copy(source, target, slab_sem.at[which]).start()
+
+    def slab_wait(which, chunk):
+        if chunk == 0:
+            own_in(which).wait()
         for k in range(1, nz):
             sender = lax.rem(mz + nz - k, nz)
-            slab_in(which, source, target, k, sender, sender).wait_recv()
+            slab_in(which, chunk, k, sender, sender).wait_recv()
+
+    for member in range(nreg):
+        block = inverses[member]
+        high = block.astype(jnp.bfloat16).astype(jnp.float32)
+        split = jnp.concatenate([high, block - high, high], axis=1)
+        weights[member * depth : (member + 1) * depth, :] = split.astype(jnp.bfloat16)
 
     blocks = inverses[...]
     scale = 1.0 / jnp.max(jnp.max(jnp.abs(blocks), axis=0), axis=(0, 1), keepdims=True)
@@ -200,7 +226,17 @@
             edges[n] = packed
             return carry
 
-        lax.fori_loop(0, rows // 2, body, 0)
+        turns = piece // (2 * UNROLL_M)
+        for chunk in range(CHUNKS):
+            if n == 0:
+                slab_wait(0, chunk)
+
+            def turn(t, carry, chunk=chunk):
+                for u in range(UNROLL_M):
+                    body(chunk * (piece // 2) + t * UNROLL_M + u, carry)
+                return carry
+
+            lax.fori_loop(0, turns, turn, 0)
         for at, (sends, _, source, target, device) in enumerate(halo(n)):
 
             @pl.when(sends)
@@ -244,12 +280,20 @@
             return tuple(old + new for old, new in zip(carry, sums))
 
         start = tuple(jnp.zeros((8, lanes), jnp.float32) for _ in range(n + 2))
-        parts = lax.fori_loop(0, rows, body, start)
+        parts = start
+        for chunk in range(CHUNKS):
+            if n == 0:
+                slab_wait(1, chunk)
+
+            def turn(t, carry, chunk=chunk):
+                for u in range(UNROLL_A):
+                    carry = body(chunk * piece + t * UNROLL_A + u, carry)
+                return carry
+
+            parts = lax.fori_loop(0, piece // UNROLL_A, turn, parts)
         return [jnp.sum(part, axis=0, keepdims=True) for part in parts]
 
-    slab_wait(0)
     precondition(0)
-    slab_wait(1)
     sums = operate(0)
     precondition(1)
     sums = sums + operate(1)
@@ -307,48 +351,66 @@
     c0 = (g0 - a01 * c1 - a02 * c2) * p0
     c0, c1, c2 = (c[0:1] for c in (c0, c1, c2))
 
-    piece = rows // CHUNKS
-    outs = ((x_z, x_out), (r_z, r_out))
-
-    def slab_out(which, chunk, k, peer, owner):
-        source, target = outs[which]
+    def mix(terms):
+        first, second, third = terms
+        return c0 * first + c1 * second + c2 * third
+
+    x_rim[0] = mix([fields[n, 0] for n in range(BASIS)])
+    x_rim[1] = mix([fields[n, rows + 1] for n in range(BASIS)])
+    x_rim[2] = mix([edges_left[n] for n in range(BASIS)])
+    x_rim[3] = mix([edges_right[n] for n in range(BASIS)])
+    x_z[0] = jnp.zeros((rows, lanes), jnp.float32)
+    x_z[depth + 1] = jnp.zeros((rows, lanes), jnp.float32)
+
+    def rim_out(k, peer, owner):
         return pltpu.make_async_remote_copy(
-            src_ref=source.at[slab_span(peer), pl.ds(chunk * piece, piece), :],
-            dst_ref=target.at[:, row_span(owner, chunk * piece, piece), :],
-            send_sem=out_send.at[which, chunk, k],
-            recv_sem=out_recv.at[which, chunk, k],
+            src_ref=x_rim.at[:, slab_span(peer), :],
+            dst_ref=rim_in.at[owner],
+            send_sem=rim_send.at[k],
+            recv_sem=rim_recv.at[k],
             device_id={"gz": peer},
             device_id_type=MESH,
         )
 
-    def keep(which, chunk):
-        source, target = outs[which]
-        return pltpu.make_async_copy(
-            source.at[slab_span(mz), pl.ds(chunk * piece, piece), :],
-            target.at[:, row_span(mz, chunk * piece, piece), :],
-            out_local.at[which, chunk],
+    def slab_out(chunk, k, peer, owner):
+        return pltpu.make_async_remote_copy(
+            src_ref=x_z.at[pl.ds(peer * slab, slab + 2), pl.ds(chunk * piece, piece), :],
+            dst_ref=x_in.at[owner, :, pl.ds(chunk * piece, piece), :],
+            send_sem=out_send.at[chunk, k],
+            recv_sem=out_recv.at[chunk, k],
+            device_id={"gz": peer},
+            device_id_type=MESH,
         )
 
     for chunk in range(CHUNKS):
 
-        def final(i, carry):
-            i = chunk * piece + i
-            span = pl.ds(i, depth, stride=rows)
-            x = c0 * fields[0, i + 1] + c1 * fields[1, i + 1] + c2 * fields[2, i + 1]
-            x_z.reshape(depth * rows, lanes)[span, :] = x
-            r = rhs_t[i] - (c0 * images[0, i] + c1 * images[1, i] + c2 * images[2, i])
-            r_z.reshape(depth * rows, lanes)[span, :] = r
+        def final(t, carry):
+            for u in range(UNROLL_F):
+                i = chunk * piece + t * UNROLL_F + u
+                x = mix([fields[n, i + 1] for n in range(BASIS)])
+                x_z.reshape((depth + 2) * rows, lanes)[pl.ds(rows + i, depth, stride=rows), :] = x
             return carry
 
-        lax.fori_loop(0, piece, final, 0)
-        for which in range(2):
+        lax.fori_loop(0, piece // UNROLL_F, final, 0)
+        for k in range(1, nz):
+            slab_out(chunk, k, lax.rem(mz + k, nz), mz).start()
+    for k in range(1, nz):
+        rim_out(k, lax.rem(mz + k, nz), mz).start()
+
+    own_x = pltpu.make_async_copy(
+        x_z.at[pl.ds(mz * slab, slab + 2)], x_in.at[mz], local_sem.at[0]
+    )
+    own_rim = pltpu.make_async_copy(
+        x_rim.at[:, slab_span(mz), :], rim_in.at[mz], local_sem.at[1]
+    )
+    own_x.start()
+    own_rim.start()
+    for which, (source, target) in enumerate(slabs):
+        pltpu.make_async_copy(source, target, slab_sem.at[which]).wait()
+    for which in range(2):
+        for chunk in range(CHUNKS):
             for k in range(1, nz):
-                slab_out(which, chunk, k, lax.rem(mz + k, nz), mz).start()
-            keep(which, chunk).start()
-
-    for which, (source, target) in enumerate(pairs):
-        for k in range(1, nz):
-            slab_in(which, source, target, k, lax.rem(mz + k, nz), mz).wait_send()
+                slab_in(which, chunk, k, lax.rem(mz + k, nz), mz).wait_send()
     for n in range(BASIS):
         for at, (sends, _, source, target, device) in enumerate(halo(n)):
 
@@ -356,13 +418,68 @@
             def _(n=n, at=at, source=source, target=target, device=device):
                 halo_copy(n, at, source, target, device).wait_send()
 
-    for which in range(2):
+    plane_lane = lax.broadcasted_iota(jnp.int32, (rows, lanes), 1)
+    plane_row = lax.broadcasted_iota(jnp.int32, (rows, lanes), 0)
+
+    def result(which, owner):
+        source = x_in.at[owner, pl.ds(1, slab)] if which == 0 else r_in.at[owner]
+        return pltpu.make_async_copy(
+            source,
+            (x_out, r_out)[which].at[:, row_span(owner, 0, rows), :],
+            out_local.at[which, owner],
+        )
+
+    def finish(owner):
+        result(0, owner).start()
+        rim = [rim_in[owner, 2], rim_in[owner, 3]]
+        rim.append(jnp.zeros((lanes - 2 * slab, lanes), jnp.float32))
+        turned = jnp.concatenate(rim, axis=0).T
+        first, last = turned[rows : 2 * rows], turned[:rows]
+        start = pl.multiple_of(place(owner) * rows, 8)
+
+        def plane(z, carry):
+            x = x_in[owner, z + 1]
+            beside = x_in[owner, z] + x_in[owner, z + 2]
+            above = jnp.broadcast_to(rim_in[owner, 0, pl.ds(z, 1), :], x.shape)
+            below = jnp.broadcast_to(rim_in[owner, 1, pl.ds(z, 1), :], x.shape)
+            beside = beside + jnp.where(plane_row == 0, above, pltpu.roll(x, 1, 0))
+            beside = beside + jnp.where(plane_row == rows - 1, below, pltpu.roll(x, rows - 1, 0))
+            from_left = pltpu.roll(first, lax.rem(lanes - z, lanes), 1)
+            from_right = pltpu.roll(last, lanes - 1 - slab - z, 1)
+            beside = beside + jnp.where(plane_lane == 0, from_left, pltpu.roll(x, 1, 1))
+            beside = beside + jnp.where(
+                plane_lane == lanes - 1, from_right, pltpu.roll(x, lanes - 1, 1)
+            )
+            image = (6.0 + diag_slab[z, pl.ds(start, rows), :]) * x - beside
+            r_in[owner, z] = rhs_slab[z, pl.ds(start, rows), :] - image
+            return carry
+
+        def turn(t, carry):
+            for u in range(UNROLL_F):
+                carry = plane(t * UNROLL_F + u, carry)
+            return carry
+
+        lax.fori_loop(0, slab // UNROLL_F, turn, 0)
+        result(1, owner).start()
+
+    own_x.wait()
+    own_rim.wait()
+    finish(mz)
+    order = sorted(range(1, nz), key=lambda k: (min(k, nz - k), k))
+    for k in order:
+        sender = lax.rem(mz + nz - k, nz)
+        rim_out(k, sender, sender).wait_recv()
         for chunk in range(CHUNKS):
-            keep(which, chunk).wait()
-            for k in range(1, nz):
-                sender = lax.rem(mz + nz - k, nz)
-                slab_out(which, chunk, k, sender, sender).wait_recv()
-                slab_out(which, chunk, k, lax.rem(mz + k, nz), mz).wait_send()
+            slab_out(chunk, k, sender, sender).wait_recv()
+        finish(sender)
+    for k in range(nz):
+        for which in range(2):
+            result(which, lax.rem(mz + k, nz)).wait()
+    for k in range(1, nz):
+        peer = lax.rem(mz + k, nz)
+        rim_out(k, peer, mz).wait_send()
+        for chunk in range(CHUNKS):
+            slab_out(chunk, k, peer, mz).wait_send()
 
 
 def per_device(sizes, right_side, diagonal, regime, inverses):
@@ -370,10 +487,6 @@
     nz = sizes["gz"]
     depth, rows = slab * nz, wide // nz
     nreg = inverses.shape[0]
-    high = lax.reduce_precision(inverses, 8, 7)
-    low = lax.reduce_precision(inverses - high, 8, 7)
-    weights = jnp.concatenate([high, low, high], axis=-1).reshape(nreg * depth, 3 * depth)
-    weights = weights.astype(jnp.bfloat16)
     column = (rows, depth, lanes)
     layered = (depth, rows, lanes)
     f32 = jnp.float32
@@ -382,11 +495,14 @@
         functools.partial(kernel, sizes),
         out_shape=[jax.ShapeDtypeStruct(right_side.shape, f32)] * 2,
         in_specs=[pl.BlockSpec(memory_space=pl.ANY)] * 2
-        + [pl.BlockSpec(memory_space=pltpu.VMEM)] * 3,
+        + [pl.BlockSpec(memory_space=pltpu.VMEM)] * 2,
         out_specs=[pl.BlockSpec(memory_space=pl.ANY)] * 2,
         scratch_shapes=[
+            pltpu.VMEM((nreg * depth, 3 * depth), jnp.bfloat16),
             pltpu.VMEM(layered, f32),
             pltpu.VMEM(layered, f32),
+            pltpu.VMEM(right_side.shape, f32),
+            pltpu.VMEM(right_side.shape, f32),
             pltpu.VMEM(column, f32),
             pltpu.VMEM(column, f32),
             pltpu.VMEM((BASIS, rows + 2, depth, lanes), f32),
@@ -394,26 +510,32 @@
             pltpu.VMEM((BASIS, depth, lanes), f32),
             pltpu.VMEM((BASIS, depth, lanes), f32),
             pltpu.VMEM((BASIS, depth, lanes), f32),
-            pltpu.VMEM(layered, f32),
-            pltpu.VMEM(layered, f32),
+            pltpu.VMEM((depth + 2, rows, lanes), f32),
+            pltpu.VMEM((4, depth, lanes), f32),
+            pltpu.VMEM((nz, slab + 2, rows, lanes), f32),
+            pltpu.VMEM((nz, 4, slab, lanes), f32),
+            pltpu.VMEM((nz, slab, rows, lanes), f32),
             pltpu.VMEM((nz, SUMS, lanes), f32),
             pltpu.VMEM((sizes["gx"], SUMS, lanes), f32),
             pltpu.VMEM((sizes["gy"], SUMS, lanes), f32),
             dma((2,)),
-            dma((2, nz)),
-            dma((2, nz)),
+            dma((2, CHUNKS, nz)),
+            dma((2, CHUNKS, nz)),
             dma((BASIS, 4)),
             dma((BASIS, 4)),
             dma((3, max(sizes.values()))),
             dma((3, max(sizes.values()))),
-            dma((2, CHUNKS, nz)),
-            dma((2, CHUNKS, nz)),
-            dma((2, CHUNKS)),
+            dma((CHUNKS, nz)),
+            dma((CHUNKS, nz)),
+            dma((2, nz)),
+            dma((nz,)),
+            dma((nz,)),
+            dma((2,)),
         ],
         compiler_params=pltpu.CompilerParams(
             collective_id=0, has_side_effects=True, vmem_limit_bytes=56 * 1024 * 1024
         ),
-    )(right_side, diagonal, regime, inverses, weights)
+    )(right_side, diagonal, regime, inverses)
 
 
 def solution(mesh):

time: 254 us -> 201 us (0.79)
  Pallas kernels: 247 us -> 195 us
    pallas_call x1, Pallas kernels: 247 us -> 195 us  [per_device(): pl.pallas_call(functools.partial(kernel, sizes), out_shape=[jax.ShapeDtyp...]
where the time goes in v2:
time: 201 us
  Pallas kernels  195 us (97%)
  local copies, waits for them, and re-layouts  4.58 us (2%)
    pallas_call x1, Pallas kernels, per_device(): pl.pallas_call(functools.partial(kernel, sizes), out_shape=[jax.ShapeDtyp...  195 us
    unnamed x4, local copies, waits for them, and re-layouts  4.58 us

profile of v2, /device:TPU:0, one launch (start us, length us, event | category | flops | bytes accessed | tf_op | source)
XLA Modules:
  0.0 200.6 jit_solution(6923693228820867330)
XLA Ops:
  0.6 195.4 %shard_map.59 = (f32[16,256,128]{2,1,0:T(8,128)}, f32[16,256,128]{2,1,0:T(8,128)}) custom-call(f32[16,256,128]{2,1,0:T(8,128)} %rhs.1, f32[16,256,128]{2,1,0:T(8,128)} %diag.1, s32[256,128]{1,0:T(8,128)} %regime.1, f32[8,64,64]{2,1,0:T(8,128)} %inverses.1), custom_call_target="tpu_custom_call" | custom-call | tf_op jit(solution)/shard_map/pallas_call | solution.py:494
  196.0 0.0 copy-start
  196.0 3.3 %copy.8 = f32[16,256,128]{2,1,0:T(8,128)} copy(f32[16,256,128]{2,1,0:T(8,128)} %get-tuple-element.4) | data formatting | bytes 4194304
  199.3 0.0 copy-done
  199.3 1.3 copy.9
Async XLA Ops:
  196.0 3.3 %copy-start = (f32[16,256,128]{2,1,0:T(8,128)S(1)}, f32[16,256,128]{2,1,0:T(8,128)}, u32[]{:S(2)}) copy-start(f32[16,256,128]{2,1,0:T(8,128)} %get-tuple-element.5) | copy-start | bytes 6291460

commit v3 on v2

--- a/solution.py
+++ b/solution.py
@@ -11,8 +11,8 @@
 BASIS = 3
 CHUNKS = 4
 SUMS = 16
-UNROLL_M = 2
-UNROLL_A = 4
+UNROLL_M = 4
+UNROLL_A = 8
 UNROLL_F = 4
 
 
@@ -186,8 +186,9 @@
             def _(target=target):
                 target[...] = zeros
 
-    def precondition(n):
-        edges[n] = zeros
+    def precondition(n, chunks, done):
+        if chunks[0] == 0:
+            edges[n] = zeros
 
         def body(b, carry):
             columns = []
@@ -227,7 +228,7 @@
             return carry
 
         turns = piece // (2 * UNROLL_M)
-        for chunk in range(CHUNKS):
+        for chunk in chunks:
             if n == 0:
                 slab_wait(0, chunk)
 
@@ -237,6 +238,8 @@
                 return carry
 
             lax.fori_loop(0, turns, turn, 0)
+        if not done:
+            return
         for at, (sends, _, source, target, device) in enumerate(halo(n)):
 
             @pl.when(sends)
@@ -291,13 +294,15 @@
                 return carry
 
             parts = lax.fori_loop(0, piece // UNROLL_A, turn, parts)
+            if n == 0:
+                precondition(1, [chunk], chunk == CHUNKS - 1)
         return [jnp.sum(part, axis=0, keepdims=True) for part in parts]
 
-    precondition(0)
+    everything = list(range(CHUNKS))
+    precondition(0, everything, True)
     sums = operate(0)
-    precondition(1)
     sums = sums + operate(1)
-    precondition(2)
+    precondition(2, everything, True)
     sums = sums + operate(2)
 
     sums.append(jnp.zeros((SUMS - len(sums), lanes), jnp.float32))

time: 201 us -> 195 us (0.970)
  Pallas kernels: 195 us -> 190 us
    pallas_call x1, Pallas kernels: 195 us -> 190 us  [per_device(): pl.pallas_call(functools.partial(kernel, sizes), out_shape=[jax.ShapeDtyp...]
where the time goes in v3:
time: 195 us
  Pallas kernels  190 us (97%)
  local copies, waits for them, and re-layouts  4.58 us (2%)
    pallas_call x1, Pallas kernels, per_device(): pl.pallas_call(functools.partial(kernel, sizes), out_shape=[jax.ShapeDtyp...  190 us
    unnamed x4, local copies, waits for them, and re-layouts  4.58 us

profile of v3, /device:TPU:0, one launch (start us, length us, event | category | flops | bytes accessed | tf_op | source)
XLA Modules:
  0.0 194.9 jit_solution(922730144735116902)
XLA Ops:
  0.6 189.7 %shard_map.59 = (f32[16,256,128]{2,1,0:T(8,128)}, f32[16,256,128]{2,1,0:T(8,128)}) custom-call(f32[16,256,128]{2,1,0:T(8,128)} %rhs.1, f32[16,256,128]{2,1,0:T(8,128)} %diag.1, s32[256,128]{1,0:T(8,128)} %regime.1, f32[8,64,64]{2,1,0:T(8,128)} %inverses.1), custom_call_target="tpu_custom_call" | custom-call | tf_op jit(solution)/shard_map/pallas_call | solution.py:499
  190.3 0.0 copy-start
  190.3 3.3 %copy.8 = f32[16,256,128]{2,1,0:T(8,128)} copy(f32[16,256,128]{2,1,0:T(8,128)} %get-tuple-element.4) | data formatting | bytes 4194304
  193.6 0.0 copy-done
  193.6 1.3 copy.9
Async XLA Ops:
  190.3 3.3 %copy-start = (f32[16,256,128]{2,1,0:T(8,128)S(1)}, f32[16,256,128]{2,1,0:T(8,128)}, u32[]{:S(2)}) copy-start(f32[16,256,128]{2,1,0:T(8,128)} %get-tuple-element.5) | copy-start | bytes 6291460
